TPU v7x, 32 devices: a whole 2x2x4 slice. The times are simulated.
32 devices in a mesh: grp: 2 (over x), ha: 16 (over z, y, core).
Axes of the slice: x: 2, y: 2, z: 4, core: 2. Of those that a mesh axis runs over, the one named last changes fastest.
Arguments:
- frames: bfloat16 [4, 16, 112, 384], P('grp', 'ha'), parts along dimension 0, may hold values from -6 to 6
- cache_first: bfloat16 [4, 16, 112, 384], P('grp', 'ha'), parts along dimension 0, may hold values from -5 to 5
- cache_second: bfloat16 [4, 16, 112, 384], P('grp', 'ha'), parts along dimension 0, may hold values from -5 to 5
- gain_first: float32 [384], replicated, may hold values from 0.1 to 1.9
- gain_second: float32 [384], replicated, may hold values from 0.1 to 1.9
- bias_first: float32 [384], replicated, may hold values from -3 to 3
- bias_second: float32 [384], replicated, may hold values from -3 to 3
- weight_first: bfloat16 [10368, 384], P(None, 'ha'), may hold values from -0.0625 to 0.0625
- weight_second: bfloat16 [10368, 384], P(None, 'ha'), may hold values from -0.0625 to 0.0625
- cotangent: bfloat16 [4, 16, 112, 384], P('grp', 'ha'), parts along dimension 0, may hold values from -6 to 6
Outputs:
- output: bfloat16 [4, 16, 112, 384], P('grp', 'ha'), parts along dimension 0
- grad_frames: bfloat16 [4, 16, 112, 384], P('grp', 'ha'), parts along dimension 0
There are 2 independent parts, one for each index of `grp`. A program takes and returns all parts, laid end to end along the dimension named above; an argument that names none is the same for every part. Nothing has to cross between parts.
All inputs are finite; a program needn't handle non-finite values.
Results may differ from a plain program's by a relative error of at most 0.006.
Values may be sent and summed in bfloat16 or wider, within the bound.
No kernel may reach another device: no remote copies, remote signals or barrier semaphores. Data moves between devices by JAX's collectives and lax.ppermute only.
A program may use at most 128 MiB of HBM per device.

v0:
```python
import jax
import jax.numpy as jnp
from jax import lax
from jax.sharding import PartitionSpec as P


def extended_2(block, sides, width):
    for axis, dim in sides:
        count = lax.axis_size(axis)
        forward = [(i, i + 1) for i in range(count - 1)]
        backward = [(target, source) for source, target in forward]
        low = lax.ppermute(
            lax.slice_in_dim(block, block.shape[dim] - width, None, axis=dim), axis, forward
        )
        high = lax.ppermute(lax.slice_in_dim(block, 0, width, axis=dim), axis, backward)
        block = jnp.concatenate([low, block, high], axis=dim)
    return block


def normed_silu(values, scales):
    mean_square = jnp.mean(values * values, axis=-1, keepdims=True)
    inverse = lax.rsqrt(mean_square + 1e-06)
    normed = values * inverse * scales
    return normed * jax.nn.sigmoid(normed)


def silu_backward(values, scales, upstream):
    mean_square = jnp.mean(values * values, axis=-1, keepdims=True)
    inverse = lax.rsqrt(mean_square + 1e-06)
    normed = values * inverse * scales
    sigmoid_value = jax.nn.sigmoid(normed)
    scaled = scales * upstream * sigmoid_value * (1.0 + normed * (1.0 - sigmoid_value))
    return inverse * scaled - values * inverse**3 * jnp.mean(
        values * scaled, axis=-1, keepdims=True
    )


def tap_patches(padded, length, rows, columns, flipped):
    pieces = []
    for frame_tap in range(3):
        for row_tap in range(3):
            for col_tap in range(3):
                if flipped:
                    frame_start, row_start, col_start = (2 - frame_tap, 2 - row_tap, 2 - col_tap)
                else:
                    frame_start, row_start, col_start = (frame_tap, row_tap, col_tap)
                pieces.append(
                    padded[
                        frame_start : frame_start + length,
                        row_start : row_start + rows,
                        col_start : col_start + columns,
                    ]
                )
    return jnp.stack(pieces, axis=3)


def local(
    frames,
    cache_first,
    cache_second,
    gain_first,
    gain_second,
    bias_first,
    bias_second,
    weight_first,
    weight_second,
    cotangent,
):
    length, rows, columns, channels = frames.shape
    kernel_one, kernel_two = (
        lax.all_gather(weight_first, "ha", axis=1, tiled=True),
        lax.all_gather(weight_second, "ha", axis=1, tiled=True),
    )
    kernel_one = kernel_one.reshape(27, channels, channels)
    inputs = frames.astype(jnp.float32)
    first_act = normed_silu(inputs, gain_first).astype(jnp.bfloat16)
    extended = jnp.concatenate([cache_first, first_act], axis=0)
    padded = extended_2(extended, (("ha", 1),), 1)
    padded = jnp.pad(padded, ((0, 0), (0, 0), (1, 1), (0, 0)))
    patches = tap_patches(padded, length, rows, columns, False)
    middle = jnp.einsum("lrwtc,tco->lrwo", patches, kernel_one, preferred_element_type=jnp.float32)
    middle = (middle + bias_first).astype(jnp.bfloat16)
    middle_float = middle.astype(jnp.float32)
    kernel_two = kernel_two.reshape(27, channels, channels)
    second_act = normed_silu(middle_float, gain_second).astype(jnp.bfloat16)
    extended = jnp.concatenate([cache_second, second_act], axis=0)
    padded = extended_2(extended, (("ha", 1),), 1)
    padded = jnp.pad(padded, ((0, 0), (0, 0), (1, 1), (0, 0)))
    patches = tap_patches(padded, length, rows, columns, False)
    second_out = jnp.einsum(
        "lrwtc,tco->lrwo", patches, kernel_two, preferred_element_type=jnp.float32
    )
    output = (inputs + second_out + bias_second).astype(jnp.bfloat16)
    padded = extended_2(cotangent, (("ha", 1),), 1)
    padded = jnp.pad(padded, ((0, 2), (0, 0), (1, 1), (0, 0)))
    patches = tap_patches(padded, length, rows, columns, True)
    grad_second = jnp.einsum(
        "lrwto,tco->lrwc", patches, kernel_two, preferred_element_type=jnp.float32
    )
    grad_middle = silu_backward(middle_float, gain_second, grad_second).astype(jnp.bfloat16)
    padded = extended_2(grad_middle, (("ha", 1),), 1)
    padded = jnp.pad(padded, ((0, 2), (0, 0), (1, 1), (0, 0)))
    patches = tap_patches(padded, length, rows, columns, True)
    grad_first = jnp.einsum(
        "lrwto,tco->lrwc", patches, kernel_one, preferred_element_type=jnp.float32
    )
    grad_frames = (
        cotangent.astype(jnp.float32) + silu_backward(inputs, gain_first, grad_first)
    ).astype(jnp.bfloat16)
    return (output, grad_frames)


def solution(mesh):
    return jax.shard_map(
        local,
        mesh=mesh,
        in_specs=(
            P("grp", "ha", None, None),
            P("grp", "ha", None, None),
            P("grp", "ha", None, None),
            P(),
            P(),
            P(),
            P(),
            P(None, "ha"),
            P(None, "ha"),
            P("grp", "ha", None, None),
        ),
        out_specs=(P("grp", "ha", None, None), P("grp", "ha", None, None)),
        check_vma=False,
    )
```

profile of v0, /device:TPU:5, one launch (start us, length us, event | category | flops | bytes accessed | tf_op | source)
XLA Modules:
  0.0 222.6 jit_solution(1379792984267743407)
XLA Ops:
  8.7 1.0 fusion.91
  9.7 1.1 fusion.99
  10.8 1.0 pad_maximum_fusion
  11.8 2.6 %collective-permute-start.1 = (bf16[4,1,112,384]{3,2,0,1:T(8,128)(2,1)S(1)}, bf16[4,1,112,384]{3,2,0,1:T(8,128)(2,1)S(1)}, u32[]{:S(2)}, u32[]{:S(2)}) collective-permute-start(bf16[4,1,112,384]{3,2,0,1:T(8,128)(2,1)S(1)} %pad_maximum_fusion), channel_id=1, source_target_pairs={{1,0},{2,1},{3,2},{4,3},{5,4},{6,5},{7,6},{8,7},{9,8},{10,9},{11,1... | collective-permute-start | bytes 1032200 | tf_op jit(solution)/shard_map/ppermute | solution.py:15
  14.4 3.9 %collective-permute-start = (bf16[4,1,112,384]{3,2,0,1:T(8,128)(2,1)S(1)}, bf16[4,1,112,384]{3,2,0,1:T(8,128)(2,1)S(1)}, u32[]{:S(2)}, u32[]{:S(2)}) collective-permute-start(bf16[4,1,112,384]{3,2,0,1:T(8,128)(2,1)S(1)} %pad_maximum_fusion), channel_id=1, source_target_pairs={{0,1},{1,2},{2,3},{3,4},{4,5},{5,6},{6,7},{7,8},{8,9},{9,10},{10,1... | collective-permute-start | bytes 1032200 | tf_op jit(solution)/shard_map/ppermute | solution.py:12
  18.3 1.9 collective-permute-start.5
  20.2 4.5 %collective-permute-start.4 = (bf16[2,1,112,384]{3,2,0,1:T(8,128)(2,1)}, bf16[2,1,112,384]{3,2,0,1:T(8,128)(2,1)S(1)}, u32[]{:S(2)}, u32[]{:S(2)}) collective-permute-start(bf16[2,1,112,384]{3,2,0,1:T(8,128)(2,1)} %bitcast.545), channel_id=1, source_target_pairs={{0,1},{1,2},{2,3},{3,4},{4,5},{5,6},{6,7},{7,8},{8,9},{9,10},{10,1... | collective-permute-start | bytes 516104 | tf_op jit(solution)/shard_map/ppermute | solution.py:12
  30.5 0.8 collective-permute-done.5
  32.9 1.1 constant_dynamic-update-slice_fusion.26
  33.9 0.8 constant_dynamic-update-slice_fusion.25
  48.8 0.9 constant_dynamic-update-slice_fusion.4
  52.5 33.8 %all-gather.3.cloned.1.call-done = bf16[10368,384]{0,1:T(8,128)(2,1)} async-done(((bf16[10368,24]{0,1:T(8,128)(2,1)}), bf16[10368,384]{0,1:T(8,128)(2,1)}) %all-gather.3.cloned.1.call-update) | async-done | bytes 7962640 | tf_op jit(solution)/shard_map/all_gather | solution.py:71
  86.2 11.3 %copy.39 = bf16[10368,384]{1,0:T(8,128)(2,1)} copy(bf16[10368,384]{0,1:T(8,128)(2,1)} %all-gather.3.cloned.1.call-done) | data formatting | bytes 15925248 | tf_op jit(solution)/shard_map/all_gather | solution.py:71
  97.6 7.4 %multiply_reduce_fusion.1 = (f32[2,112]{1,0:T(2,128)S(1)}, f32[2,112,384]{2,1,0:T(8,128)S(1)}) fusion(f32[384]{0:T(512)S(1)} %copy-done.7, bf16[27,384,384,1]{2,1,0,3:T(8,128)(2,1)} %bitcast.528, bf16[2,1,112,27,384]{4,2,3,0,1:T(8,128)(2,1)} %constant_dynamic-update-slice_fusion), kind=kOutput, calls=%fused_computation.90 | convolution fusion | flops 1784057600 | bytes 12953984 | tf_op jit(solution)/shard_map/lrwtc,tco->lrwo/dot_general | solution.py:81
  105.0 53.7 %all-gather.5.cloned.1.call-done = bf16[10368,384]{0,1:T(8,128)(2,1)} async-done(((bf16[10368,24]{0,1:T(8,128)(2,1)}), bf16[10368,384]{0,1:T(8,128)(2,1)}) %all-gather.5.cloned.1.call-update) | async-done | bytes 7962640 | tf_op jit(solution)/shard_map/all_gather | solution.py:72
  158.7 11.3 %copy.41 = bf16[10368,384]{1,0:T(8,128)(2,1)} copy(bf16[10368,384]{0,1:T(8,128)(2,1)} %all-gather.5.cloned.1.call-done) | data formatting | bytes 15925248 | tf_op jit(solution)/shard_map/all_gather | solution.py:72
  170.0 7.7 %multiply_reduce_fusion = (f32[2,112]{1,0:T(2,128)S(1)}, f32[2,112,384]{2,1,0:T(8,128)S(1)}) fusion(f32[2,112,384]{2,1,0:T(8,128)S(1)} %get-tuple-element.11, f32[2,112]{1,0:T(2,128)S(1)} %get-tuple-element.9, bf16[27,384,384,1]{2,1,3,0:T(8,128)(2,1)} %bitcast.524, bf16[2,1,112,27,384]{4,2,0,3,1:T(8,128)(2,1)} %copy-done.5, f32[384]{0:T(512)S(1)} %copy-done.6), kind=kOutput, calls=%fused_computation.86 | convolution fusion | flops 1784745728 | bytes 13298944 | tf_op jit(solution)/shard_map/lrwto,tco->lrwc/dot_general | solution.py:97
  178.0 2.2 collective-permute-start.7
  180.2 4.3 %collective-permute-start.6 = (bf16[2,1,112,384]{3,2,0,1:T(8,128)(2,1)S(1)}, bf16[2,1,112,384]{3,2,0,1:T(8,128)(2,1)S(1)}, u32[]{:S(2)}, u32[]{:S(2)}) collective-permute-start(bf16[2,1,112,384]{3,2,0,1:T(8,128)(2,1)S(1)} %bitcast.542), channel_id=1, source_target_pairs={{0,1},{1,2},{2,3},{3,4},{4,5},{5,6},{6,7},{7,8},{8,9},{9,10},{10,1... | collective-permute-start | bytes 516104 | tf_op jit(solution)/shard_map/ppermute | solution.py:12
  185.2 1.9 collective-permute-start.3
  187.1 4.7 %collective-permute-start.2 = (bf16[4,1,112,384]{3,2,0,1:T(8,128)(2,1)S(1)}, bf16[4,1,112,384]{3,2,0,1:T(8,128)(2,1)S(1)}, u32[]{:S(2)}, u32[]{:S(2)}) collective-permute-start(bf16[4,1,112,384]{3,2,0,1:T(8,128)(2,1)S(1)} %pad_maximum_fusion.1), channel_id=1, source_target_pairs={{0,1},{1,2},{2,3},{3,4},{4,5},{5,6},{6,7},{7,8},{8,9},{9,10},{10,1... | collective-permute-start | bytes 1032200 | tf_op jit(solution)/shard_map/ppermute | solution.py:12
  204.7 5.4 %fusion.105 = (f32[2,112]{1,0:T(2,128)S(1)}, f32[2,1,112,384]{3,2,0,1:T(8,128)S(1)}) fusion(bf16[2,1,112,384]{3,2,1,0:T(8,128)(2,1)S(1)} %copy-done, f32[384]{0:T(512)S(1)} %copy-done.4, f32[2,112]{1,0:T(2,128)S(1)} %get-tuple-element.7, bf16[27,384,384,1]{2,1,3,0:T(8,128)(2,1)S(1)} %bitcast.531, ...), kind=kOutput, calls=%fused_computation.84 | convolution fusion | flops 1784831744 | bytes 13126912 | tf_op jit(solution)/shard_map/lrwto,tco->lrwc/dot_general | solution.py:104
  210.0 0.8 fusion.106
  212.5 3.3 %fusion.68 = bf16[2,1,112,384]{3,2,1,0:T(8,128)(2,1)} fusion(bf16[27,384,384,1]{2,1,3,0:T(8,128)(2,1)S(1)} %bitcast.527, bf16[2,1,112,27,384]{4,2,0,3,1:T(8,128)(2,1)S(1)} %constant_dynamic-update-slice_fusion.27, bf16[2,1,112,384]{3,2,1,0:T(8,128)(2,1)S(1)} %copy-done, f32[384]{0:T(512)S(1)} %copy-done.8), kind=kOutput, calls=%fused_computation.37 | convolution fusion | flops 1783971840 | bytes 12953088 | tf_op jit(solution)/shard_map/lrwtc,tco->lrwo/dot_general | solution.py:90
  (154 shorter events, 40.5 us)
Async XLA Ops:
  7.2 24.3 %copy-start.3 = (bf16[2,1,112,384]{3,2,1,0:T(8,128)(2,1)S(1)}, bf16[2,1,112,384]{3,2,1,0:T(8,128)(2,1)}, u32[]{:S(2)}) copy-start(bf16[2,1,112,384]{3,2,1,0:T(8,128)(2,1)} %param.19) | copy-start | bytes 516100
  7.2 79.1 %all-gather.3.cloned.1.call-start = ((), (), s32[]{:S(2)}) async-start(), calls=%async_computation | async-start | bytes 8460288 | tf_op jit(solution)/shard_map/all_gather | solution.py:71
  7.9 150.8 %all-gather.5.cloned.1.call-start = ((), (), s32[]{:S(2)}) async-start(), calls=%async_computation.1 | async-start | bytes 8460288 | tf_op jit(solution)/shard_map/all_gather | solution.py:72
  11.8 20.7 %collective-permute-start.1 = (bf16[4,1,112,384]{3,2,0,1:T(8,128)(2,1)S(1)}, bf16[4,1,112,384]{3,2,0,1:T(8,128)(2,1)S(1)}, u32[]{:S(2)}, u32[]{:S(2)}) collective-permute-start(bf16[4,1,112,384]{3,2,0,1:T(8,128)(2,1)S(1)} %pad_maximum_fusion), channel_id=1, source_target_pairs={{1,0},{2,1},{3,2},{4,3},{5,4},{6,5},{7,6},{8,7},{9,8},{10,9},{11,1... | collective-permute-start | bytes 1032200 | tf_op jit(solution)/shard_map/ppermute | solution.py:15
  14.4 18.2 %collective-permute-start = (bf16[4,1,112,384]{3,2,0,1:T(8,128)(2,1)S(1)}, bf16[4,1,112,384]{3,2,0,1:T(8,128)(2,1)S(1)}, u32[]{:S(2)}, u32[]{:S(2)}) collective-permute-start(bf16[4,1,112,384]{3,2,0,1:T(8,128)(2,1)S(1)} %pad_maximum_fusion), channel_id=1, source_target_pairs={{0,1},{1,2},{2,3},{3,4},{4,5},{5,6},{6,7},{7,8},{8,9},{9,10},{10,1... | collective-permute-start | bytes 1032200 | tf_op jit(solution)/shard_map/ppermute | solution.py:12
  18.3 13.0 %collective-permute-start.5 = (bf16[2,1,112,384]{3,2,0,1:T(8,128)(2,1)}, bf16[2,1,112,384]{3,2,0,1:T(8,128)(2,1)S(1)}, u32[]{:S(2)}, u32[]{:S(2)}) collective-permute-start(bf16[2,1,112,384]{3,2,0,1:T(8,128)(2,1)} %bitcast.544), channel_id=1, source_target_pairs={{1,0},{2,1},{3,2},{4,3},{5,4},{6,5},{7,6},{8,7},{9,8},{10,9},{11,1... | collective-permute-start | bytes 516104 | tf_op jit(solution)/shard_map/ppermute | solution.py:15
  20.2 11.2 %collective-permute-start.4 = (bf16[2,1,112,384]{3,2,0,1:T(8,128)(2,1)}, bf16[2,1,112,384]{3,2,0,1:T(8,128)(2,1)S(1)}, u32[]{:S(2)}, u32[]{:S(2)}) collective-permute-start(bf16[2,1,112,384]{3,2,0,1:T(8,128)(2,1)} %bitcast.545), channel_id=1, source_target_pairs={{0,1},{1,2},{2,3},{3,4},{4,5},{5,6},{6,7},{7,8},{8,9},{9,10},{10,1... | collective-permute-start | bytes 516104 | tf_op jit(solution)/shard_map/ppermute | solution.py:12
  25.6 6.9 %copy-start.1 = (bf16[2,1,112,384]{3,2,1,0:T(8,128)(2,1)S(1)}, bf16[2,1,112,384]{3,2,1,0:T(8,128)(2,1)}, u32[]{:S(2)}) copy-start(bf16[2,1,112,384]{3,2,1,0:T(8,128)(2,1)} %param.11) | copy-start | bytes 516100
  32.5 15.6 %copy-start.5 = (bf16[2,1,112,27,384]{4,2,0,3,1:T(8,128)(2,1)}, bf16[2,1,112,27,384]{4,2,0,3,1:T(8,128)(2,1)S(1)}, u32[]{:S(2)}) copy-start(bf16[2,1,112,27,384]{4,2,0,3,1:T(8,128)(2,1)S(1)} %constant_dynamic-update-slice_fusion.54) | copy-start | bytes 13934596
  32.5 16.3 %copy-start = (bf16[2,1,112,384]{3,2,1,0:T(8,128)(2,1)S(1)}, bf16[2,1,112,384]{3,2,1,0:T(8,128)(2,1)}, u32[]{:S(2)}) copy-start(bf16[2,1,112,384]{3,2,1,0:T(8,128)(2,1)} %param.10) | copy-start | bytes 516100
  32.5 16.3 %copy-start.4 = (f32[384]{0:T(512)S(1)}, f32[384]{0:T(512)}, u32[]{:S(2)}) copy-start(f32[384]{0:T(512)} %param.13) | copy-start | bytes 4612
  52.5 45.1 %copy-start.7 = (f32[384]{0:T(512)S(1)}, f32[384]{0:T(512)}, u32[]{:S(2)}) copy-start(f32[384]{0:T(512)} %param.15) | copy-start | bytes 4612
  105.0 65.0 %copy-start.6 = (f32[384]{0:T(512)S(1)}, f32[384]{0:T(512)}, u32[]{:S(2)}) copy-start(f32[384]{0:T(512)} %param.14) | copy-start | bytes 4612
  170.0 34.7 %slice-start.2 = ((s8[7962624]{0:T(1024)(128)(4,1)}), s8[4194304]{0:T(1024)(128)(4,1)S(1)}, s32[]{:S(2)}) async-start(s8[7962624]{0:T(1024)(128)(4,1)} %bitcast.529), calls=%async_computation.4 | async-start | bytes 8388608
  170.0 15.2 %copy-start.2 = (bf16[2,1,112,384]{3,2,1,0:T(8,128)(2,1)S(1)}, bf16[2,1,112,384]{3,2,1,0:T(8,128)(2,1)}, u32[]{:S(2)}) copy-start(bf16[2,1,112,384]{3,2,1,0:T(8,128)(2,1)} %param.12) | copy-start | bytes 516100
  170.0 34.6 %slice-start.3 = ((s8[7962624]{0:T(1024)(128)(4,1)}), s8[3768320]{0:T(1024)(128)(4,1)S(1)}, s32[]{:S(2)}) async-start(s8[7962624]{0:T(1024)(128)(4,1)} %bitcast.529), calls=%async_computation.5 | async-start | bytes 7536640
  178.0 13.9 %collective-permute-start.7 = (bf16[2,1,112,384]{3,2,0,1:T(8,128)(2,1)S(1)}, bf16[2,1,112,384]{3,2,0,1:T(8,128)(2,1)S(1)}, u32[]{:S(2)}, u32[]{:S(2)}) collective-permute-start(bf16[2,1,112,384]{3,2,0,1:T(8,128)(2,1)S(1)} %bitcast.541), channel_id=1, source_target_pairs={{1,0},{2,1},{3,2},{4,3},{5,4},{6,5},{7,6},{8,7},{9,8},{10,9},{11,1... | collective-permute-start | bytes 516104 | tf_op jit(solution)/shard_map/ppermute | solution.py:15
  180.2 11.7 %collective-permute-start.6 = (bf16[2,1,112,384]{3,2,0,1:T(8,128)(2,1)S(1)}, bf16[2,1,112,384]{3,2,0,1:T(8,128)(2,1)S(1)}, u32[]{:S(2)}, u32[]{:S(2)}) collective-permute-start(bf16[2,1,112,384]{3,2,0,1:T(8,128)(2,1)S(1)} %bitcast.542), channel_id=1, source_target_pairs={{0,1},{1,2},{2,3},{3,4},{4,5},{5,6},{6,7},{7,8},{8,9},{9,10},{10,1... | collective-permute-start | bytes 516104 | tf_op jit(solution)/shard_map/ppermute | solution.py:12
  185.2 25.7 %collective-permute-start.3 = (bf16[4,1,112,384]{3,2,0,1:T(8,128)(2,1)S(1)}, bf16[4,1,112,384]{3,2,0,1:T(8,128)(2,1)S(1)}, u32[]{:S(2)}, u32[]{:S(2)}) collective-permute-start(bf16[4,1,112,384]{3,2,0,1:T(8,128)(2,1)S(1)} %pad_maximum_fusion.1), channel_id=1, source_target_pairs={{1,0},{2,1},{3,2},{4,3},{5,4},{6,5},{7,6},{8,7},{9,8},{10,9},{11,1... | collective-permute-start | bytes 1032200 | tf_op jit(solution)/shard_map/ppermute | solution.py:15
  187.1 23.8 %collective-permute-start.2 = (bf16[4,1,112,384]{3,2,0,1:T(8,128)(2,1)S(1)}, bf16[4,1,112,384]{3,2,0,1:T(8,128)(2,1)S(1)}, u32[]{:S(2)}, u32[]{:S(2)}) collective-permute-start(bf16[4,1,112,384]{3,2,0,1:T(8,128)(2,1)S(1)} %pad_maximum_fusion.1), channel_id=1, source_target_pairs={{0,1},{1,2},{2,3},{3,4},{4,5},{5,6},{6,7},{7,8},{8,9},{9,10},{10,1... | collective-permute-start | bytes 1032200 | tf_op jit(solution)/shard_map/ppermute | solution.py:12
  204.6 7.8 %slice-start = ((s8[7962624]{0:T(1024)(128)(4,1)}), s8[4194304]{0:T(1024)(128)(4,1)S(1)}, s32[]{:S(2)}) async-start(s8[7962624]{0:T(1024)(128)(4,1)} %bitcast.525), calls=%async_computation.2 | async-start | bytes 8388608
  204.6 7.8 %slice-start.1 = ((s8[7962624]{0:T(1024)(128)(4,1)}), s8[3768320]{0:T(1024)(128)(4,1)S(1)}, s32[]{:S(2)}) async-start(s8[7962624]{0:T(1024)(128)(4,1)} %bitcast.525), calls=%async_computation.3 | async-start | bytes 7536640
  211.2 1.2 copy-start.8
Sparse Core Ops, SparseCore 0:
  10.2 76.0 all-gather.2
  88.4 70.2 all-gather.4
where the time goes:
time: 223 us
  waiting for transfers between devices  89.8 us (40%)
  local copies, waits for them, and re-layouts  61.4 us (28%)
  starting transfers between devices  26.1 us (12%)
  matrix products  23.8 us (11%)
  between operations  14.6 us (7%)
  other arithmetic  6.78 us (3%)
    all_gather x1, waiting for transfers between devices, local(): lax.all_gather(weight_second, 'ha', axis=1, tiled=True)  53.7 us
    unnamed x127, local copies, waits for them, and re-layouts  37.3 us
    all_gather x1, waiting for transfers between devices, local(): lax.all_gather(weight_first, 'ha', axis=1, tiled=True)  33.8 us
    ppermute x4, starting transfers between devices, extended_2(): lax.ppermute(lax.slice_in_dim(block, block.shape[dim] - width, None, axis...  17.4 us
    all_gather x1, local copies, waits for them, and re-layouts, local(): lax.all_gather(weight_first, 'ha', axis=1, tiled=True)  11.3 us
    all_gather x1, local copies, waits for them, and re-layouts, local(): lax.all_gather(weight_second, 'ha', axis=1, tiled=True)  11.3 us
    ppermute x4, starting transfers between devices, extended_2(): lax.ppermute(lax.slice_in_dim(block, 0, width, axis=dim), axis, backward)  8.6 us
    dot_general x1, matrix products, local(): jnp.einsum('lrwto,tco->lrwc', patches, kernel_two, preferred_element_type...  7.75 us
  transfers between devices with their start and end apart: 10, of which 4 were waited for; matrix products, arithmetic and copies ran while one was open for 31% of the time, Pallas kernels for 0%

commit v1 on v0

--- a/solution.py
+++ b/solution.py
@@ -2,6 +2,13 @@
 import jax.numpy as jnp
 from jax import lax
 from jax.sharding import PartitionSpec as P
+
+
+def all_by_exchange(x, axis, dim):
+    n_dev = lax.axis_size(axis)
+    tiles = jnp.stack([x for _ in range(n_dev)])
+    tiles = lax.all_to_all(tiles, axis, split_axis=0, concat_axis=0)
+    return jnp.concatenate(tiles, axis=dim)
 
 
 def extended_2(block, sides, width):
@@ -68,7 +75,7 @@
 ):
     length, rows, columns, channels = frames.shape
     kernel_one, kernel_two = (
-        lax.all_gather(weight_first, "ha", axis=1, tiled=True),
+        all_by_exchange(weight_first, "ha", 1),
         lax.all_gather(weight_second, "ha", axis=1, tiled=True),
     )
     kernel_one = kernel_one.reshape(27, channels, channels)

time: 223 us -> 369 us (1.65)
  the two profiles are of different devices: /device:TPU:5 before, /device:TPU:16 now
where the time goes in v1:
time: 369 us; the launch traced here: 368 us
  waiting for transfers between devices  208 us (56%)
  local copies, waits for them, and re-layouts  81.6 us (22%)
  starting transfers between devices  32.7 us (9%)
  matrix products  26.9 us (7%)
  between operations  14.7 us (4%)
  other arithmetic  4.06 us (1%)
    ppermute x4, waiting for transfers between devices, extended_2(): lax.ppermute(lax.slice_in_dim(block, block.shape[dim] - width, None, axis...  207 us
    unnamed x129, local copies, waits for them, and re-layouts  37.2 us
    another operation x2, local copies, waits for them, and re-layouts, local(): kernel_one = kernel_one.reshape(27, channels, channels)  26.9 us
    ppermute x4, starting transfers between devices, extended_2(): lax.ppermute(lax.slice_in_dim(block, 0, width, axis=dim), axis, backward)  18.2 us
    all_gather x1, local copies, waits for them, and re-layouts, local(): lax.all_gather(weight_second, 'ha', axis=1, tiled=True)  11.3 us
    dot_general x1, matrix products, local(): jnp.einsum('lrwto,tco->lrwc', patches, kernel_one, preferred_element_type...  8.51 us
    ppermute x4, starting transfers between devices, extended_2(): lax.ppermute(lax.slice_in_dim(block, block.shape[dim] - width, None, axis...  8.05 us
    dot_general x1, matrix products, local(): jnp.einsum('lrwto,tco->lrwc', patches, kernel_two, preferred_element_type...  7.72 us
  transfers between devices with their start and end apart: 10, of which 1 were waited for; matrix products, arithmetic and copies ran while one was open for 23% of the time, Pallas kernels for 0%

profile of v1, /device:TPU:16, one launch (start us, length us, event | category | flops | bytes accessed | tf_op | source)
XLA Modules:
  0.0 367.5 jit_solution(12871437953055186392)
XLA Ops:
  7.2 4.6 %stack.349 = bf16[16,10368,24]{1,2,0:T(8,128)(2,1)} broadcast(bf16[10368,24]{0,1:T(8,128)(2,1)} %param.17), dimensions={1,2} | broadcast | bytes 8460288 | tf_op jit(solution)/shard_map/stack | solution.py:9
  11.8 6.3 %all-to-all-start = ((bf16[16,10368,24]{1,2,0:T(8,128)(2,1)}), bf16[16,10368,24]{1,2,0:T(8,128)(2,1)}, u32[]{:S(2)}, u32[]{:S(2)}) async-start(bf16[16,10368,24]{1,2,0:T(8,128)(2,1)} %stack.349), calls=%async_computation | async-start | bytes 15925248 | tf_op jit(solution)/shard_map/all_to_all | solution.py:10
  19.3 2.0 collective-permute-start
  21.3 4.4 %collective-permute-start.1 = (bf16[4,1,112,384]{3,2,0,1:T(8,128)(2,1)S(1)}, bf16[4,1,112,384]{3,2,0,1:T(8,128)(2,1)S(1)}, u32[]{:S(2)}, u32[]{:S(2)}) collective-permute-start(bf16[4,1,112,384]{3,2,0,1:T(8,128)(2,1)S(1)} %pad_maximum_fusion), channel_id=1, source_target_pairs={{1,0},{2,1},{3,2},{4,3},{5,4},{6,5},{7,6},{8,7},{9,8},{10,9},{11,1... | collective-permute-start | bytes 1032200 | tf_op jit(solution)/shard_map/ppermute | solution.py:22
  25.8 1.9 collective-permute-start.4
  27.7 4.5 %collective-permute-start.5 = (bf16[2,1,112,384]{3,2,0,1:T(8,128)(2,1)S(1)}, bf16[2,1,112,384]{3,2,0,1:T(8,128)(2,1)S(1)}, u32[]{:S(2)}, u32[]{:S(2)}) collective-permute-start(bf16[2,1,112,384]{3,2,0,1:T(8,128)(2,1)S(1)} %bitcast.554), channel_id=1, source_target_pairs={{1,0},{2,1},{3,2},{4,3},{5,4},{6,5},{7,6},{8,7},{9,8},{10,9},{11,1... | collective-permute-start | bytes 516104 | tf_op jit(solution)/shard_map/ppermute | solution.py:22
  38.0 207.0 %collective-permute-done.4 = bf16[2,1,112,384]{3,2,0,1:T(8,128)(2,1)S(1)} collective-permute-done((bf16[2,1,112,384]{3,2,0,1:T(8,128)(2,1)S(1)}, bf16[2,1,112,384]{3,2,0,1:T(8,128)(2,1)S(1)}, u32[]{:S(2)}, u32[]{:S(2)}) %collective-permute-start.4) | collective-permute-done | bytes 172064 | tf_op jit(solution)/shard_map/ppermute | solution.py:19
  246.4 1.0 constant_dynamic-update-slice_fusion.26
  247.4 0.9 constant_dynamic-update-slice_fusion.25
  258.8 0.7 constant_dynamic-update-slice_fusion.9
  262.3 0.9 constant_dynamic-update-slice_fusion.4
  266.0 13.8 %reshape_reshape.3 = bf16[27,384,384]{1,0,2:T(8,128)(2,1)} reshape(bf16[10368,16,24]{0,2,1:T(8,128)(2,1)} %bitcast.56) | data formatting | bytes 15925248 | tf_op jit(solution)/shard_map/reshape;reshape | solution.py:81
  279.7 13.1 %copy.78 = bf16[27,384,384]{2,1,0:T(8,128)(2,1)} copy(bf16[27,384,384]{1,0,2:T(8,128)(2,1)} %reshape_reshape.3) | data formatting | bytes 15925248 | tf_op jit(solution)/shard_map/reshape;reshape | solution.py:81
  292.8 7.4 %multiply_reduce_fusion.1 = (f32[2,112]{1,0:T(2,128)S(1)}, f32[2,112,384]{2,1,0:T(8,128)S(1)}) fusion(f32[384]{0:T(512)S(1)} %copy-done.7, bf16[27,384,384]{2,1,0:T(8,128)(2,1)} %copy.78, bf16[2,1,112,27,384]{4,2,3,0,1:T(8,128)(2,1)} %constant_dynamic-update-slice_fusion), kind=kOutput, calls=%fused_computation.92 | convolution fusion | flops 1784057600 | bytes 12953984 | tf_op jit(solution)/shard_map/lrwtc,tco->lrwo/dot_general | solution.py:88
  300.3 11.3 %copy.80 = bf16[10368,384]{1,0:T(8,128)(2,1)} copy(bf16[10368,384]{0,1:T(8,128)(2,1)} %all-gather.2.cloned.1.call-done) | data formatting | bytes 15925248 | tf_op jit(solution)/shard_map/all_gather | solution.py:79
  311.6 7.7 %multiply_reduce_fusion = (f32[2,112]{1,0:T(2,128)S(1)}, f32[2,112,384]{2,1,0:T(8,128)S(1)}) fusion(f32[2,112,384]{2,1,0:T(8,128)S(1)} %get-tuple-element.13, f32[2,112]{1,0:T(2,128)S(1)} %get-tuple-element.11, bf16[27,384,384,1]{2,1,3,0:T(8,128)(2,1)} %bitcast.537, bf16[2,1,112,27,384]{4,2,0,3,1:T(8,128)(2,1)} %copy-done.5, f32[384]{0:T(512)S(1)} %copy-done.6), kind=kOutput, calls=%fused_computation.88 | convolution fusion | flops 1784745728 | bytes 13298944 | tf_op jit(solution)/shard_map/lrwto,tco->lrwc/dot_general | solution.py:104
  319.6 2.2 collective-permute-start.6
  321.8 4.5 %collective-permute-start.7 = (bf16[2,1,112,384]{3,2,0,1:T(8,128)(2,1)S(1)}, bf16[2,1,112,384]{3,2,0,1:T(8,128)(2,1)S(1)}, u32[]{:S(2)}, u32[]{:S(2)}) collective-permute-start(bf16[2,1,112,384]{3,2,0,1:T(8,128)(2,1)S(1)} %bitcast.551), channel_id=1, source_target_pairs={{1,0},{2,1},{3,2},{4,3},{5,4},{6,5},{7,6},{8,7},{9,8},{10,9},{11,1... | collective-permute-start | bytes 516104 | tf_op jit(solution)/shard_map/ppermute | solution.py:22
  327.0 1.9 collective-permute-start.2
  329.0 4.7 %collective-permute-start.3 = (bf16[4,1,112,384]{3,2,0,1:T(8,128)(2,1)S(1)}, bf16[4,1,112,384]{3,2,0,1:T(8,128)(2,1)S(1)}, u32[]{:S(2)}, u32[]{:S(2)}) collective-permute-start(bf16[4,1,112,384]{3,2,0,1:T(8,128)(2,1)S(1)} %pad_maximum_fusion.1), channel_id=1, source_target_pairs={{1,0},{2,1},{3,2},{4,3},{5,4},{6,5},{7,6},{8,7},{9,8},{10,9},{11,1... | collective-permute-start | bytes 1032200 | tf_op jit(solution)/shard_map/ppermute | solution.py:22
  338.1 0.7 constant_dynamic-update-slice_fusion.92
  346.5 8.5 %fusion.125 = (f32[2,112]{1,0:T(2,128)S(1)}, f32[2,1,112,384]{3,2,0,1:T(8,128)S(1)}) fusion(bf16[2,1,112,384]{3,2,1,0:T(8,128)(2,1)S(1)} %copy-done, f32[384]{0:T(512)S(1)} %copy-done.4, f32[2,112]{1,0:T(2,128)S(1)} %get-tuple-element.9, bf16[27,384,384,1]{1,0,2,3:T(8,128)(2,1)S(1)} %bitcast.536, ...), kind=kOutput, calls=%fused_computation.86 | convolution fusion | flops 1784831744 | bytes 13126912 | tf_op jit(solution)/shard_map/lrwto,tco->lrwc/dot_general | solution.py:111
  355.0 0.8 fusion.126
  357.4 3.3 fusion.88
  (157 shorter events, 38.4 us)
Async XLA Ops:
  11.8 7.1 %copy-start = (bf16[2,1,112,384]{3,2,1,0:T(8,128)(2,1)S(1)}, bf16[2,1,112,384]{3,2,1,0:T(8,128)(2,1)}, u32[]{:S(2)}) copy-start(bf16[2,1,112,384]{3,2,1,0:T(8,128)(2,1)} %param.10) | copy-start | bytes 516100
  11.8 7.2 %copy-start.4 = (f32[384]{0:T(512)S(1)}, f32[384]{0:T(512)}, u32[]{:S(2)}) copy-start(f32[384]{0:T(512)} %param.13) | copy-start | bytes 4612
  11.8 7.4 %copy-start.1 = (bf16[2,1,112,384]{3,2,1,0:T(8,128)(2,1)S(1)}, bf16[2,1,112,384]{3,2,1,0:T(8,128)(2,1)}, u32[]{:S(2)}) copy-start(bf16[2,1,112,384]{3,2,1,0:T(8,128)(2,1)} %param.11) | copy-start | bytes 516100
  11.8 13.9 %copy-start.3 = (bf16[2,1,112,384]{3,2,1,0:T(8,128)(2,1)S(1)}, bf16[2,1,112,384]{3,2,1,0:T(8,128)(2,1)}, u32[]{:S(2)}) copy-start(bf16[2,1,112,384]{3,2,1,0:T(8,128)(2,1)} %param.19) | copy-start | bytes 516100
  11.8 254.1 %all-to-all-start = ((bf16[16,10368,24]{1,2,0:T(8,128)(2,1)}), bf16[16,10368,24]{1,2,0:T(8,128)(2,1)}, u32[]{:S(2)}, u32[]{:S(2)}) async-start(bf16[16,10368,24]{1,2,0:T(8,128)(2,1)} %stack.349), calls=%async_computation | async-start | bytes 15925248 | tf_op jit(solution)/shard_map/all_to_all | solution.py:10
  18.1 282.1 %all-gather.2.cloned.1.call-start = ((), (), s32[]{:S(2)}) async-start(), calls=%async_computation.1 | async-start | bytes 8460288 | tf_op jit(solution)/shard_map/all_gather | solution.py:79
  19.3 226.8 %collective-permute-start = (bf16[4,1,112,384]{3,2,0,1:T(8,128)(2,1)S(1)}, bf16[4,1,112,384]{3,2,0,1:T(8,128)(2,1)S(1)}, u32[]{:S(2)}, u32[]{:S(2)}) collective-permute-start(bf16[4,1,112,384]{3,2,0,1:T(8,128)(2,1)S(1)} %pad_maximum_fusion), channel_id=1, source_target_pairs={{0,1},{1,2},{2,3},{3,4},{4,5},{5,6},{6,7},{7,8},{8,9},{9,10},{10,1... | collective-permute-start | bytes 1032200 | tf_op jit(solution)/shard_map/ppermute | solution.py:19
  21.3 224.8 %collective-permute-start.1 = (bf16[4,1,112,384]{3,2,0,1:T(8,128)(2,1)S(1)}, bf16[4,1,112,384]{3,2,0,1:T(8,128)(2,1)S(1)}, u32[]{:S(2)}, u32[]{:S(2)}) collective-permute-start(bf16[4,1,112,384]{3,2,0,1:T(8,128)(2,1)S(1)} %pad_maximum_fusion), channel_id=1, source_target_pairs={{1,0},{2,1},{3,2},{4,3},{5,4},{6,5},{7,6},{8,7},{9,8},{10,9},{11,1... | collective-permute-start | bytes 1032200 | tf_op jit(solution)/shard_map/ppermute | solution.py:22
  25.8 219.2 %collective-permute-start.4 = (bf16[2,1,112,384]{3,2,0,1:T(8,128)(2,1)S(1)}, bf16[2,1,112,384]{3,2,0,1:T(8,128)(2,1)S(1)}, u32[]{:S(2)}, u32[]{:S(2)}) collective-permute-start(bf16[2,1,112,384]{3,2,0,1:T(8,128)(2,1)S(1)} %bitcast.553), channel_id=1, source_target_pairs={{0,1},{1,2},{2,3},{3,4},{4,5},{5,6},{6,7},{7,8},{8,9},{9,10},{10,1... | collective-permute-start | bytes 516104 | tf_op jit(solution)/shard_map/ppermute | solution.py:19
  27.7 217.3 %collective-permute-start.5 = (bf16[2,1,112,384]{3,2,0,1:T(8,128)(2,1)S(1)}, bf16[2,1,112,384]{3,2,0,1:T(8,128)(2,1)S(1)}, u32[]{:S(2)}, u32[]{:S(2)}) collective-permute-start(bf16[2,1,112,384]{3,2,0,1:T(8,128)(2,1)S(1)} %bitcast.554), channel_id=1, source_target_pairs={{1,0},{2,1},{3,2},{4,3},{5,4},{6,5},{7,6},{8,7},{9,8},{10,9},{11,1... | collective-permute-start | bytes 516104 | tf_op jit(solution)/shard_map/ppermute | solution.py:22
  246.0 15.6 %copy-start.5 = (bf16[2,1,112,27,384]{4,2,0,3,1:T(8,128)(2,1)}, bf16[2,1,112,27,384]{4,2,0,3,1:T(8,128)(2,1)S(1)}, u32[]{:S(2)}) copy-start(bf16[2,1,112,27,384]{4,2,0,3,1:T(8,128)(2,1)S(1)} %constant_dynamic-update-slice_fusion.54) | copy-start | bytes 13934596
  279.7 13.1 %copy-start.7 = (f32[384]{0:T(512)S(1)}, f32[384]{0:T(512)}, u32[]{:S(2)}) copy-start(f32[384]{0:T(512)} %param.15) | copy-start | bytes 4612
  300.2 11.4 %copy-start.6 = (f32[384]{0:T(512)S(1)}, f32[384]{0:T(512)}, u32[]{:S(2)}) copy-start(f32[384]{0:T(512)} %param.14) | copy-start | bytes 4612
  311.6 15.4 %copy-start.2 = (bf16[2,1,112,384]{3,2,1,0:T(8,128)(2,1)S(1)}, bf16[2,1,112,384]{3,2,1,0:T(8,128)(2,1)}, u32[]{:S(2)}) copy-start(bf16[2,1,112,384]{3,2,1,0:T(8,128)(2,1)} %param.12) | copy-start | bytes 516100
  311.6 34.8 %slice-start = ((s8[9437184]{0:T(1024)(128)(4,1)}), s8[4194304]{0:T(1024)(128)(4,1)S(1)}, s32[]{:S(2)}) async-start(s8[9437184]{0:T(1024)(128)(4,1)} %bitcast.534), calls=%async_computation.2 | async-start | bytes 8388608
  311.6 34.8 %slice-start.1 = ((s8[9437184]{0:T(1024)(128)(4,1)}), s8[1048576]{0:T(1024)(128)(4,1)S(1)}, s32[]{:S(2)}) async-start(s8[9437184]{0:T(1024)(128)(4,1)} %bitcast.534), calls=%async_computation.3 | async-start | bytes 2097152
  319.6 26.9 %slice-start.2 = ((s8[9437184]{0:T(1024)(128)(4,1)}), s8[4194304]{0:T(1024)(128)(4,1)S(1)}, s32[]{:S(2)}) async-start(s8[9437184]{0:T(1024)(128)(4,1)} %bitcast.534), calls=%async_computation.4 | async-start | bytes 8388608
  319.6 14.1 %collective-permute-start.6 = (bf16[2,1,112,384]{3,2,0,1:T(8,128)(2,1)S(1)}, bf16[2,1,112,384]{3,2,0,1:T(8,128)(2,1)S(1)}, u32[]{:S(2)}, u32[]{:S(2)}) collective-permute-start(bf16[2,1,112,384]{3,2,0,1:T(8,128)(2,1)S(1)} %bitcast.550), channel_id=1, source_target_pairs={{0,1},{1,2},{2,3},{3,4},{4,5},{5,6},{6,7},{7,8},{8,9},{9,10},{10,1... | collective-permute-start | bytes 516104 | tf_op jit(solution)/shard_map/ppermute | solution.py:19
  321.8 11.9 %collective-permute-start.7 = (bf16[2,1,112,384]{3,2,0,1:T(8,128)(2,1)S(1)}, bf16[2,1,112,384]{3,2,0,1:T(8,128)(2,1)S(1)}, u32[]{:S(2)}, u32[]{:S(2)}) collective-permute-start(bf16[2,1,112,384]{3,2,0,1:T(8,128)(2,1)S(1)} %bitcast.551), channel_id=1, source_target_pairs={{1,0},{2,1},{3,2},{4,3},{5,4},{6,5},{7,6},{8,7},{9,8},{10,9},{11,1... | collective-permute-start | bytes 516104 | tf_op jit(solution)/shard_map/ppermute | solution.py:22
  327.0 28.8 %collective-permute-start.2 = (bf16[4,1,112,384]{3,2,0,1:T(8,128)(2,1)S(1)}, bf16[4,1,112,384]{3,2,0,1:T(8,128)(2,1)S(1)}, u32[]{:S(2)}, u32[]{:S(2)}) collective-permute-start(bf16[4,1,112,384]{3,2,0,1:T(8,128)(2,1)S(1)} %pad_maximum_fusion.1), channel_id=1, source_target_pairs={{0,1},{1,2},{2,3},{3,4},{4,5},{5,6},{6,7},{7,8},{8,9},{9,10},{10,1... | collective-permute-start | bytes 1032200 | tf_op jit(solution)/shard_map/ppermute | solution.py:19
  329.0 26.9 %collective-permute-start.3 = (bf16[4,1,112,384]{3,2,0,1:T(8,128)(2,1)S(1)}, bf16[4,1,112,384]{3,2,0,1:T(8,128)(2,1)S(1)}, u32[]{:S(2)}, u32[]{:S(2)}) collective-permute-start(bf16[4,1,112,384]{3,2,0,1:T(8,128)(2,1)S(1)} %pad_maximum_fusion.1), channel_id=1, source_target_pairs={{1,0},{2,1},{3,2},{4,3},{5,4},{6,5},{7,6},{8,7},{9,8},{10,9},{11,1... | collective-permute-start | bytes 1032200 | tf_op jit(solution)/shard_map/ppermute | solution.py:22
  346.4 10.9 %slice-start.3 = ((s8[7962624]{0:T(1024)(128)(4,1)}), s8[4194304]{0:T(1024)(128)(4,1)S(1)}, s32[]{:S(2)}) async-start(s8[7962624]{0:T(1024)(128)(4,1)} %bitcast.538), calls=%async_computation.5 | async-start | bytes 8388608
  346.5 10.9 %slice-start.4 = ((s8[7962624]{0:T(1024)(128)(4,1)}), s8[3768320]{0:T(1024)(128)(4,1)S(1)}, s32[]{:S(2)}) async-start(s8[7962624]{0:T(1024)(128)(4,1)} %bitcast.538), calls=%async_computation.6 | async-start | bytes 7536640
  356.2 1.2 copy-start.8
Sparse Core Ops, SparseCore 0:
  21.1 171.0 all-gather.1
